TPU v7x, 256 devices: a whole 4x4x8 slice. The times are simulated.
256 devices in a mesh: band: 64 (over z, y, core), field: 4 (over x).
Axes of the slice: x: 4, y: 4, z: 8, core: 2. Of those that a mesh axis runs over, the one named last changes fastest.
Arguments:
- right_side: float32 [640, 2, 4, 12, 640], P('band', None, 'field'), may hold values from -40 to 40
- legendre: bfloat16 [640, 640, 640], P('band'), may hold values from -0.25 to 0.25
- wave_map: int32 [640], replicated, may hold values from 0 to 639, as said below
- obs_weight: float32 [640, 1280], P('band'), may hold values from 0.2 to 5
Outputs:
- solution: float32 [640, 2, 4, 12, 640], P('band', None, 'field')
- residual: float32 [640, 2, 4, 12, 640], P('band', None, 'field')
Inputs may be any that keep to these rules, and one draw needn't show every extreme that they name: A permutation of 0 to 639; wave_map[s] lies in the same aligned block of 20 values as 639-s.
All inputs are finite; a program needn't handle non-finite values.
Results may differ from a plain program's by a relative error of at most 0.03.
Values may be sent and summed in bfloat16 or wider, within the bound.
No kernel may reach another device: no remote copies, remote signals or barrier semaphores. Data moves between devices by JAX's collectives and lax.ppermute only.
A program may use at most 128 MiB of HBM per device.

v0:
```python
import functools
import math
import jax
import jax.numpy as jnp
from jax import lax
from jax.sharding import Mesh
from jax.sharding import PartitionSpec as P

ITERS = 3
BAND_FIELD = ("band_0", "band_1", "band_2", "field")
BAND = ("band_0", "band_1", "band_2")


def by_axis(array, axes):
    return functools.reduce(lax.psum, axes, array)


def triangle_of(own_waves, degrees):
    return (jnp.arange(degrees, dtype=jnp.int32)[None, :] >= own_waves[:, None]).astype(jnp.float32)


def fourier_of(wave_map, lon_count):
    longitude = jnp.arange(lon_count, dtype=jnp.int32)
    phase_int = wave_map[:, None] * longitude[None, :] % lon_count
    angles = phase_int.astype(jnp.float32) * (2.0 * math.pi / lon_count)
    norm_factor = 1.0 / math.sqrt(wave_map.shape[0])
    return (jnp.stack([jnp.cos(angles), -jnp.sin(angles)], axis=1) * norm_factor).astype(
        jnp.bfloat16
    )


def grid_round(spread, fourier_flat, obs_weight):
    slots, parts, items, single, lat_rows = spread.shape
    flat = spread.reshape(slots * parts, items * single * lat_rows)
    grid_vals = lax.dot_general(
        flat, fourier_flat, (((0,), (0,)), ((), ())), preferred_element_type=jnp.float32
    )
    grid_vals = (
        grid_vals.reshape(items * single, lat_rows, fourier_flat.shape[1]) * obs_weight[None, :, :]
    )
    weighted = grid_vals.astype(jnp.bfloat16).reshape(
        items * single * lat_rows, fourier_flat.shape[1]
    )
    returned = lax.dot_general(
        fourier_flat, weighted, (((1,), (1,)), ((), ())), preferred_element_type=jnp.float32
    ).astype(jnp.bfloat16)
    return returned.reshape(slots, parts, items, single, lat_rows)


def legendre_back(returned, legendre):
    return lax.dot_general(
        returned, legendre, (((4,), (2,)), ((0,), (0,))), preferred_element_type=jnp.float32
    )


def paired_sums(residual, image_vec):
    return (
        by_axis(jnp.sum(residual * residual), BAND_FIELD),
        by_axis(jnp.sum(residual * image_vec), BAND_FIELD),
    )


def on_device(right_side, legendre, wave_map, obs_weight):
    slot_count = legendre.shape[0]
    band_count = lax.axis_size(BAND)
    lat_rows = obs_weight.shape[0]
    first_slot = lax.axis_index(BAND) * slot_count
    own_waves = lax.dynamic_slice_in_dim(wave_map, first_slot, slot_count)
    triangle = triangle_of(own_waves, right_side.shape[4])
    fourier_table = fourier_of(wave_map, obs_weight.shape[1])
    fourier_flat = fourier_table.reshape(2 * fourier_table.shape[0], fourier_table.shape[2])
    triangle_five = triangle[:, None, None, None, :]
    field_count = right_side.shape[2]
    level_count = right_side.shape[3]
    merged = field_count * level_count

    def operate(vector):
        masked_bf = (vector * triangle_five).astype(jnp.bfloat16)
        coeffs = lax.dot_general(
            masked_bf, legendre, (((4,), (1,)), ((0,), (0,))), preferred_element_type=jnp.float32
        ).astype(jnp.bfloat16)
        outgoing = coeffs.reshape(slot_count, 2, merged, band_count, lat_rows)
        spread = lax.all_to_all(outgoing, BAND, split_axis=3, concat_axis=0, tiled=True)
        returned = grid_round(spread, fourier_flat, obs_weight)
        returned_home = lax.all_to_all(returned, BAND, split_axis=0, concat_axis=3, tiled=True)
        home = returned_home.reshape(slot_count, 2, field_count, level_count, band_count * lat_rows)
        adjoint = legendre_back(home, legendre)
        return vector + triangle_five * adjoint

    residual = right_side * triangle_five
    solution = jnp.zeros_like(residual)
    image_vec = operate(residual)
    norm_now, product = paired_sums(residual, image_vec)
    step_length = norm_now / product
    direction = residual
    along = image_vec
    for iteration in range(ITERS):
        solution = solution + step_length * direction
        residual = residual - step_length * along
        if iteration + 1 < ITERS:
            image_vec = operate(residual)
            norm_next, product = paired_sums(residual, image_vec)
            beta_ratio = norm_next / norm_now
            step_length = norm_next / (product - beta_ratio * norm_next / step_length)
            direction = residual + beta_ratio * direction
            along = image_vec + beta_ratio * along
            norm_now = norm_next
    return (solution, residual)


def solution(mesh):
    split = Mesh(
        mesh.devices.reshape(8, 4, 2, mesh.shape["field"]), ("band_0", "band_1", "band_2", "field")
    )
    return jax.shard_map(
        on_device,
        mesh=split,
        in_specs=(P(BAND, None, "field", None, None), P(BAND, None, None), P(), P(BAND, None)),
        out_specs=(P(BAND, None, "field", None, None), P(BAND, None, "field", None, None)),
        check_vma=False,
    )
```

profile of v0, /device:TPU:32, one launch (start us, length us, event | category | flops | bytes accessed | tf_op | source)
XLA Modules:
  0.0 736.9 jit_solution(9783474237335254011)
XLA Ops:
  1.5 4.9 fusion.49
  6.4 9.7 %reshape.240 = bf16[10,2,12,64,10]{4,3,2,1,0:T(8,128)(2,1)} reshape(bf16[10,2,12,640]{3,2,1,0:T(8,128)(2,1)S(1)} %fusion.49) | data formatting | bytes 614400 | tf_op jit(solution)/shard_map/reshape | solution.py:82
  16.1 14.1 %copy.117 = bf16[10,2,12,64,10]{2,1,4,0,3:T(2,128)(2,1)S(1)} copy(bf16[10,2,12,64,10]{4,3,2,1,0:T(8,128)(2,1)} %reshape.240) | data formatting | bytes 614400 | tf_op jit(solution)/shard_map/reshape | solution.py:82
  30.2 4.4 reshape.247
  34.6 12.1 %all-to-all-start = ((bf16[64,2,1200]{2,1,0:T(2,128)(2,1)}), bf16[64,2,1200]{2,1,0:T(2,128)(2,1)}, u32[]{:S(2)}, u32[]{:S(2)}) async-start(bf16[64,2,1200]{2,1,0:T(2,128)(2,1)} %reshape.247), calls=%async_computation | async-start | bytes 655360 | tf_op jit(solution)/shard_map/all_to_all | solution.py:83
  46.7 13.8 %fusion.17 = (f32[640,1,1280]{2,0,1:T(8,128)S(1)}, f32[640,1,1280]{2,0,1:T(8,128)S(1)}) fusion(s32[640]{0:T(1024)S(1)} %copy-done.2), kind=kLoop, calls=%fused_computation.21 | loop fusion | flops 8192000 | bytes 6556160 | tf_op jit(solution)/shard_map/cos | solution.py:27
  71.2 7.8 %reshape.248 = bf16[64,10,10,2,12]{4,3,2,1,0:T(2,128)(2,1)S(1)} reshape(bf16[64,2,1200]{2,1,0:T(2,128)(2,1)} %all-to-all-done) | data formatting | bytes 614400
  79.0 4.0 bitcast_bitcast_fusion.2
  83.1 13.4 %copy.118 = bf16[64,10,2,12,1,10]{5,3,2,1,0,4:T(8,128)(2,1)} copy(bf16[64,10,2,12,1,10]{3,2,5,1,0,4:T(2,128)(2,1)} %bitcast_bitcast_fusion.2) | data formatting | bytes 614400 | tf_op jit(solution)/shard_map/all_to_all | solution.py:83
  96.4 6.4 reshape.222
  113.7 5.8 reshape.224
  119.5 12.1 %copy.123 = bf16[640,2,12,1,10]{2,1,4,3,0:T(2,128)(2,1)S(1)} copy(bf16[640,2,12,1,10]{4,2,1,0,3:T(8,128)(2,1)} %reshape.224) | data formatting | bytes 614400 | tf_op jit(solution)/shard_map/reshape | solution.py:47
  131.6 4.4 reshape.249
  136.0 23.7 %all_to_all.90 = bf16[64,2,1200]{2,1,0:T(2,128)(2,1)} all-to-all(bf16[64,2,1200]{2,1,0:T(2,128)(2,1)} %reshape.249), channel_id=1, replica_groups=mesh['band_0'=8,'band_1'=4,'band_2'=2,'field'=4] {'band_0','band_1','ban..., dimensions={0} | all-to-all | bytes 614400 | tf_op jit(solution)/shard_map/all_to_all | solution.py:85
  159.7 7.8 %reshape.250 = bf16[640,1,10,2,12]{4,3,2,1,0:T(2,128)(2,1)S(1)} reshape(bf16[64,2,1200]{2,1,0:T(2,128)(2,1)} %all_to_all.90) | data formatting | bytes 614400
  167.5 17.5 %copy.154 = bf16[64,10,2,12,1,10]{1,0,2,5,3,4:T(8,128)(2,1)} copy(bf16[64,10,2,12,1,10]{3,2,5,1,0,4:T(2,128)(2,1)S(1)} %bitcast.136) | data formatting | bytes 614400 | tf_op jit(solution)/shard_map/all_to_all | solution.py:85
  185.0 12.6 %copy.155 = bf16[10,2,12,64,1,10]{5,3,2,1,0,4:T(8,128)(2,1)} copy(bf16[10,2,12,64,1,10]{0,3,1,5,2,4:T(8,128)(2,1)} %bitcast.132) | data formatting | bytes 614400 | tf_op jit(solution)/shard_map/reshape.6
  197.7 6.7 reshape.242
  204.3 6.5 fusion.66
  210.8 16.0 %all-reduce.2 = (f32[]{:T(128)}, f32[]{:T(128)}) all-reduce(f32[]{:T(128)} %get-tuple-element.17, f32[]{:T(128)} %get-tuple-element.16), channel_id=1, replica_groups=mesh['band_0'=8,'band_1'=4,'band_2'=2,'field'=4] {'band_0'}, use_global_device_ids=true, to_apply=%region_1.2 | all-reduce | flops 2 | bytes 16 | tf_op jit(solution)/shard_map/psum | solution.py:15
  226.8 10.6 %all-reduce.8 = (f32[]{:T(128)}, f32[]{:T(128)}) all-reduce(f32[]{:T(128)} %get-tuple-element.22, f32[]{:T(128)} %get-tuple-element.23), channel_id=1, replica_groups=mesh['band_0'=8,'band_1'=4,'band_2'=2,'field'=4] {'band_1'}, use_global_device_ids=true, to_apply=%region_2.3 | all-reduce | flops 2 | bytes 16 | tf_op jit(solution)/shard_map/psum | solution.py:15
  240.5 11.4 %all-reduce.5 = (f32[]{:T(128)}, f32[]{:T(128)}) all-reduce(f32[]{:T(128)} %get-tuple-element.40, f32[]{:T(128)} %get-tuple-element.41), channel_id=1, replica_groups=mesh['band_0'=8,'band_1'=4,'band_2'=2,'field'=4] {'field'}, use_global_device_ids=true, to_apply=%region_4.5 | all-reduce | flops 2 | bytes 16 | tf_op jit(solution)/shard_map/psum | solution.py:15
  253.4 4.7 fusion.52
  258.1 9.7 %reshape.243 = bf16[10,2,12,64,10]{4,3,2,1,0:T(8,128)(2,1)} reshape(bf16[10,2,12,640]{3,2,1,0:T(8,128)(2,1)S(1)} %fusion.52) | data formatting | bytes 614400 | tf_op jit(solution)/shard_map/reshape | solution.py:82
  267.8 14.6 %copy.128 = bf16[10,2,12,64,10]{2,1,4,0,3:T(2,128)(2,1)} copy(bf16[10,2,12,64,10]{4,3,2,1,0:T(8,128)(2,1)} %reshape.243) | data formatting | bytes 614400 | tf_op jit(solution)/shard_map/reshape | solution.py:82
  282.4 7.0 reshape.251
  289.4 19.6 %all_to_all.91 = bf16[64,2,1200]{2,1,0:T(2,128)(2,1)S(1)} all-to-all(bf16[64,2,1200]{2,1,0:T(2,128)(2,1)S(1)} %reshape.251), channel_id=1, replica_groups=mesh['band_0'=8,'band_1'=4,'band_2'=2,'field'=4] {'band_0','band_1','ban..., dimensions={0} | all-to-all | bytes 614400 | tf_op jit(solution)/shard_map/all_to_all | solution.py:83
  309.0 3.9 reshape.252
  312.9 5.9 bitcast_bitcast_fusion.1
  318.8 13.2 %copy.129 = bf16[64,10,2,12,1,10]{5,3,2,1,0,4:T(8,128)(2,1)} copy(bf16[64,10,2,12,1,10]{3,2,5,1,0,4:T(2,128)(2,1)} %bitcast_bitcast_fusion.1) | data formatting | bytes 614400 | tf_op jit(solution)/shard_map/all_to_all | solution.py:83
  332.0 6.4 reshape.228
  347.5 5.7 reshape.230
  353.3 12.7 %copy.134 = bf16[640,2,12,1,10]{2,1,4,3,0:T(2,128)(2,1)} copy(bf16[640,2,12,1,10]{4,2,1,0,3:T(8,128)(2,1)} %reshape.230) | data formatting | bytes 614400 | tf_op jit(solution)/shard_map/reshape | solution.py:47
  365.9 7.0 reshape.253
  372.9 19.2 %all_to_all.92 = bf16[64,2,1200]{2,1,0:T(2,128)(2,1)S(1)} all-to-all(bf16[64,2,1200]{2,1,0:T(2,128)(2,1)S(1)} %reshape.253), channel_id=1, replica_groups=mesh['band_0'=8,'band_1'=4,'band_2'=2,'field'=4] {'band_0','band_1','ban..., dimensions={0} | all-to-all | bytes 614400 | tf_op jit(solution)/shard_map/all_to_all | solution.py:85
  392.1 3.9 reshape.254
  396.0 15.4 %copy.158 = bf16[64,10,2,12,1,10]{1,0,2,5,3,4:T(8,128)(2,1)} copy(bf16[64,10,2,12,1,10]{3,2,5,1,0,4:T(2,128)(2,1)} %bitcast.138) | data formatting | bytes 614400 | tf_op jit(solution)/shard_map/all_to_all | solution.py:85
  411.4 12.6 %copy.159 = bf16[10,2,12,64,1,10]{5,3,2,1,0,4:T(8,128)(2,1)} copy(bf16[10,2,12,64,1,10]{0,3,1,5,2,4:T(8,128)(2,1)} %bitcast.133) | data formatting | bytes 614400 | tf_op jit(solution)/shard_map/reshape.12
  424.1 6.6 reshape.244
  430.7 7.4 %multiply_reduce_fusion.2 = (f32[]{:T(128)}, f32[]{:T(128)}, f32[10,2,1,12,640]{4,3,1,0,2:T(8,128)}) fusion(f32[10,2,1,12,640]{4,3,1,0,2:T(8,128)S(1)} %fusion.59, bf16[10,2,12,640]{3,2,1,0:T(8,128)(2,1)S(1)} %reshape.244, bf16[10,640,640]{2,1,0:T(8,128)(2,1)} %param.5, f32[10,640]{1,0:T(8,128)S(1)} %fusion.82), kind=kOutput, calls=%fused_computation.63 | convolution fusion | flops 197529600 | bytes 9753608 | tf_op jit(solution)/shard_map/dot_general | solution.py:51
  438.2 16.1 %all-reduce.1 = (f32[]{:T(128)}, f32[]{:T(128)}) all-reduce(f32[]{:T(128)} %get-tuple-element.15, f32[]{:T(128)} %get-tuple-element.14), channel_id=1, replica_groups=mesh['band_0'=8,'band_1'=4,'band_2'=2,'field'=4] {'band_0'}, use_global_device_ids=true, to_apply=%region_11.12 | all-reduce | flops 2 | bytes 16 | tf_op jit(solution)/shard_map/psum | solution.py:15
  454.2 10.6 %all-reduce.7 = (f32[]{:T(128)}, f32[]{:T(128)}) all-reduce(f32[]{:T(128)} %get-tuple-element.20, f32[]{:T(128)} %get-tuple-element.21), channel_id=1, replica_groups=mesh['band_0'=8,'band_1'=4,'band_2'=2,'field'=4] {'band_1'}, use_global_device_ids=true, to_apply=%region_12.13 | all-reduce | flops 2 | bytes 16 | tf_op jit(solution)/shard_map/psum | solution.py:15
  468.0 8.4 %all-reduce.4 = (f32[]{:T(128)}, f32[]{:T(128)}) all-reduce(f32[]{:T(128)} %get-tuple-element.38, f32[]{:T(128)} %get-tuple-element.39), channel_id=1, replica_groups=mesh['band_0'=8,'band_1'=4,'band_2'=2,'field'=4] {'field'}, use_global_device_ids=true, to_apply=%region_14.15 | all-reduce | flops 2 | bytes 16 | tf_op jit(solution)/shard_map/psum | solution.py:15
  482.2 5.5 fusion.55
  487.7 10.4 %reshape.245 = bf16[10,2,12,64,10]{4,3,2,1,0:T(8,128)(2,1)} reshape(bf16[10,2,12,640]{3,2,1,0:T(8,128)(2,1)} %fusion.55) | data formatting | bytes 614400 | tf_op jit(solution)/shard_map/reshape | solution.py:82
  498.1 14.6 %copy.139 = bf16[10,2,12,64,10]{2,1,4,0,3:T(2,128)(2,1)} copy(bf16[10,2,12,64,10]{4,3,2,1,0:T(8,128)(2,1)} %reshape.245) | data formatting | bytes 614400 | tf_op jit(solution)/shard_map/reshape | solution.py:82
  512.6 7.6 %reshape.255 = bf16[64,2,1200]{2,1,0:T(2,128)(2,1)} reshape(bf16[64,10,10,2,12]{4,3,2,1,0:T(2,128)(2,1)} %bitcast.139) | data formatting | bytes 614400
  520.3 19.6 %all_to_all.93 = bf16[64,2,1200]{2,1,0:T(2,128)(2,1)} all-to-all(bf16[64,2,1200]{2,1,0:T(2,128)(2,1)} %reshape.255), channel_id=1, replica_groups=mesh['band_0'=8,'band_1'=4,'band_2'=2,'field'=4] {'band_0','band_1','ban..., dimensions={0} | all-to-all | bytes 614400 | tf_op jit(solution)/shard_map/all_to_all | solution.py:83
  539.9 8.6 %reshape.256 = bf16[64,10,10,2,12]{4,3,2,1,0:T(2,128)(2,1)} reshape(bf16[64,2,1200]{2,1,0:T(2,128)(2,1)} %all_to_all.93) | data formatting | bytes 614400
  548.5 5.9 bitcast_bitcast_fusion
  554.4 13.2 %copy.140 = bf16[64,10,2,12,1,10]{5,3,2,1,0,4:T(8,128)(2,1)} copy(bf16[64,10,2,12,1,10]{3,2,5,1,0,4:T(2,128)(2,1)} %bitcast_bitcast_fusion) | data formatting | bytes 614400 | tf_op jit(solution)/shard_map/all_to_all | solution.py:83
  567.7 7.1 reshape.234
  589.7 6.7 reshape.236
  596.3 12.7 %copy.145 = bf16[640,2,12,1,10]{2,1,4,3,0:T(2,128)(2,1)} copy(bf16[640,2,12,1,10]{4,2,1,0,3:T(8,128)(2,1)} %reshape.236) | data formatting | bytes 614400 | tf_op jit(solution)/shard_map/reshape | solution.py:47
  609.0 7.6 %reshape.257 = bf16[64,2,1200]{2,1,0:T(2,128)(2,1)} reshape(bf16[640,1,10,2,12]{4,3,2,1,0:T(2,128)(2,1)} %bitcast.143) | data formatting | bytes 614400
  616.6 19.6 %all_to_all.94 = bf16[64,2,1200]{2,1,0:T(2,128)(2,1)} all-to-all(bf16[64,2,1200]{2,1,0:T(2,128)(2,1)} %reshape.257), channel_id=1, replica_groups=mesh['band_0'=8,'band_1'=4,'band_2'=2,'field'=4] {'band_0','band_1','ban..., dimensions={0} | all-to-all | bytes 614400 | tf_op jit(solution)/shard_map/all_to_all | solution.py:85
  636.2 8.6 %reshape.258 = bf16[640,1,10,2,12]{4,3,2,1,0:T(2,128)(2,1)} reshape(bf16[64,2,1200]{2,1,0:T(2,128)(2,1)} %all_to_all.94) | data formatting | bytes 614400
  644.8 15.4 %copy.162 = bf16[64,10,2,12,1,10]{1,0,2,5,3,4:T(8,128)(2,1)} copy(bf16[64,10,2,12,1,10]{3,2,5,1,0,4:T(2,128)(2,1)} %bitcast.140) | data formatting | bytes 614400 | tf_op jit(solution)/shard_map/all_to_all | solution.py:85
  660.3 12.7 %copy.163 = bf16[10,2,12,64,1,10]{5,3,2,1,0,4:T(8,128)(2,1)} copy(bf16[10,2,12,64,1,10]{0,3,1,5,2,4:T(8,128)(2,1)} %bitcast.134) | data formatting | bytes 614400 | tf_op jit(solution)/shard_map/reshape.18
  672.9 7.3 reshape.246
  680.2 7.6 %multiply_reduce_fusion = (f32[]{:T(128)}, f32[]{:T(128)}, f32[10,2,1,12,640]{4,3,1,0,2:T(8,128)}) fusion(f32[10,2,1,12,640]{4,3,1,0,2:T(8,128)S(1)} %multiply_subtract_fusion.1, bf16[10,2,12,640]{3,2,1,0:T(8,128)(2,1)} %reshape.246, bf16[10,640,640]{2,1,0:T(8,128)(2,1)} %param.5, f32[10,640]{1,0:T(8,128)S(1)} %fusion.82), kind=kOutput, calls=%fused_computation.58 | convolution fusion | flops 197529600 | bytes 9753608 | tf_op jit(solution)/shard_map/dot_general | solution.py:51
  687.8 16.0 %all-reduce = (f32[]{:T(128)}, f32[]{:T(128)}) all-reduce(f32[]{:T(128)} %get-tuple-element.13, f32[]{:T(128)} %get-tuple-element.12), channel_id=1, replica_groups=mesh['band_0'=8,'band_1'=4,'band_2'=2,'field'=4] {'band_0'}, use_global_device_ids=true, to_apply=%region_21.22 | all-reduce | flops 2 | bytes 16 | tf_op jit(solution)/shard_map/psum | solution.py:15
  703.8 10.6 %all-reduce.6 = (f32[]{:T(128)}, f32[]{:T(128)}) all-reduce(f32[]{:T(128)} %get-tuple-element.18, f32[]{:T(128)} %get-tuple-element.19), channel_id=1, replica_groups=mesh['band_0'=8,'band_1'=4,'band_2'=2,'field'=4] {'band_1'}, use_global_device_ids=true, to_apply=%region_22.23 | all-reduce | flops 2 | bytes 16 | tf_op jit(solution)/shard_map/psum | solution.py:15
  717.4 10.3 %all-reduce.3 = (f32[]{:T(128)}, f32[]{:T(128)}) all-reduce(f32[]{:T(128)} %get-tuple-element.36, f32[]{:T(128)} %get-tuple-element.37), channel_id=1, replica_groups=mesh['band_0'=8,'band_1'=4,'band_2'=2,'field'=4] {'field'}, use_global_device_ids=true, to_apply=%region_24.25 | all-reduce | flops 2 | bytes 16 | tf_op jit(solution)/shard_map/psum | solution.py:15
  (44 shorter events, 61.9 us)
Async XLA Ops:
  30.2 16.6 %copy-start.2 = (s32[640]{0:T(1024)S(1)}, s32[640]{0:T(1024)}, u32[]{:S(2)}) copy-start(s32[640]{0:T(1024)} %param.6) | copy-start | bytes 7684
  34.6 36.6 %all-to-all-start = ((bf16[64,2,1200]{2,1,0:T(2,128)(2,1)}), bf16[64,2,1200]{2,1,0:T(2,128)(2,1)}, u32[]{:S(2)}, u32[]{:S(2)}) async-start(bf16[64,2,1200]{2,1,0:T(2,128)(2,1)} %reshape.247), calls=%async_computation | async-start | bytes 655360 | tf_op jit(solution)/shard_map/all_to_all | solution.py:83
  96.4 7.5 %copy-start.3 = (f32[10,1280]{1,0:T(8,128)S(1)}, f32[10,1280]{1,0:T(8,128)}, u32[]{:S(2)}) copy-start(f32[10,1280]{1,0:T(8,128)} %param.7) | copy-start | bytes 153604
  103.9 5.7 copy-start.1
  197.6 6.7 copy-start
where the time goes:
time: 747 us; the launch traced here: 737 us
  local copies, waits for them, and re-layouts  419 us (56%)
  blocking collectives  221 us (30%)
  matrix products  55.6 us (7%)
  other arithmetic  18 us (2%)
  starting transfers between devices  12.1 us (2%)
  between operations  11.1 us (1%)
    psum x12, blocking collectives, by_axis(): return functools.reduce(lax.psum, axes, array)  119 us
    unnamed x22, local copies, waits for them, and re-layouts  81.6 us
    reshape x6, local copies, waits for them, and re-layouts, operate(): outgoing = coeffs.reshape(slot_count, 2, merged, band_count, lat_rows)  73.1 us
    all_to_all x3, blocking collectives, operate(): lax.all_to_all(returned, BAND, split_axis=0, concat_axis=3, tiled=True)  62.5 us
    another operation x6, local copies, waits for them, and re-layouts  58.5 us
    all_to_all x6, local copies, waits for them, and re-layouts, operate(): lax.all_to_all(outgoing, BAND, split_axis=3, concat_axis=0, tiled=True)  55.7 us
    reshape x6, local copies, waits for them, and re-layouts, grid_round(): return returned.reshape(slots, parts, items, single, lat_rows)  55.6 us
    all_to_all x3, local copies, waits for them, and re-layouts, operate(): lax.all_to_all(returned, BAND, split_axis=0, concat_axis=3, tiled=True)  48.3 us
  transfers between devices with their start and end apart: 1, of which 0 were waited for; matrix products, arithmetic and copies ran while one was open for 3% of the time, Pallas kernels for 0%

commit v1 on v0

--- a/solution.py
+++ b/solution.py
@@ -82,7 +82,10 @@
         outgoing = coeffs.reshape(slot_count, 2, merged, band_count, lat_rows)
         spread = lax.all_to_all(outgoing, BAND, split_axis=3, concat_axis=0, tiled=True)
         returned = grid_round(spread, fourier_flat, obs_weight)
-        returned_home = lax.all_to_all(returned, BAND, split_axis=0, concat_axis=3, tiled=True)
+        returned_home = jnp.concatenate(
+            lax.all_to_all(jnp.stack(jnp.split(returned, lax.axis_size(BAND), axis=0)), BAND, 0, 0),
+            axis=3,
+        )
         home = returned_home.reshape(slot_count, 2, field_count, level_count, band_count * lat_rows)
         adjoint = legendre_back(home, legendre)
         return vector + triangle_five * adjoint

time: 747 us -> 1100 us (1.47)
  local copies, waits for them, and re-layouts: 419 us -> 765 us
    unnamed x22 -> x381, local copies, waits for them, and re-layouts: 81.6 us -> 243 us
    another operation x6 -> x204, local copies, waits for them, and re-layouts: 58.5 us -> 217 us  [the longest x198 152 us: operate(): jnp.stack(jnp.split(returned, lax.axis_size(BAND), axis=0))]
    split x0 -> x204, local copies, waits for them, and re-layouts: none -> 114 us  [operate(): jnp.split(returned, lax.axis_size(BAND), axis=0)]
    all_to_all x3 -> x0, local copies, waits for them, and re-layouts: 48.3 us -> none  [operate(): lax.all_to_all(returned, BAND, split_axis=0, concat_axis=3, tiled=True)]
    reshape x6 -> x3, local copies, waits for them, and re-layouts: 55.6 us -> 15.7 us  [operate(): jnp.concatenate(lax.all_to_all(jnp.stack(jnp.split(returned, lax.axis_siz...]
  transfers between devices with their start and end apart: 1 -> 1, of which waited for: 0 -> 0; matrix products, arithmetic and copies ran while one was open for 3% -> 2% of each run, Pallas kernels for 0% -> 0%
where the time goes in v1:
time: 1100 us; the launch traced here: 1080 us
  local copies, waits for them, and re-layouts  765 us (70%)
  blocking collectives  220 us (20%)
  matrix products  53.2 us (5%)
  other arithmetic  17.8 us (2%)
  starting transfers between devices  12.1 us (1%)
  between operations  12 us (1%)
    unnamed x381, local copies, waits for them, and re-layouts  243 us
    another operation x198, local copies, waits for them, and re-layouts, operate(): jnp.stack(jnp.split(returned, lax.axis_size(BAND), axis=0))  152 us
    psum x12, blocking collectives, by_axis(): return functools.reduce(lax.psum, axes, array)  119 us
    split x204, local copies, waits for them, and re-layouts, operate(): jnp.split(returned, lax.axis_size(BAND), axis=0)  114 us
    reshape x6, local copies, waits for them, and re-layouts, operate(): outgoing = coeffs.reshape(slot_count, 2, merged, band_count, lat_rows)  73 us
    another operation x6, local copies, waits for them, and re-layouts  64.8 us
    all_to_all x3, blocking collectives, operate(): lax.all_to_all(jnp.stack(jnp.split(returned, lax.axis_size(BAND), axis=0)...  61.9 us
    all_to_all x6, local copies, waits for them, and re-layouts, operate(): lax.all_to_all(outgoing, BAND, split_axis=3, concat_axis=0, tiled=True)  55.7 us
  transfers between devices with their start and end apart: 1, of which 0 were waited for; matrix products, arithmetic and copies ran while one was open for 2% of the time, Pallas kernels for 0%

profile of v1, /device:TPU:32, one launch (start us, length us, event | category | flops | bytes accessed | tf_op | source)
XLA Modules:
  0.0 1079.9 jit_solution(12090406999082745719)
XLA Ops:
  1.5 4.9 fusion.49
  6.4 9.7 reshape.621
  16.1 14.1 %copy.1089 = bf16[10,2,12,64,10]{2,1,4,0,3:T(2,128)(2,1)S(1)} copy(bf16[10,2,12,64,10]{4,3,2,1,0:T(8,128)(2,1)} %reshape.621) | data formatting | bytes 614400 | tf_op jit(solution)/shard_map/reshape | solution.py:82
  30.2 4.4 reshape.628
  34.6 12.1 %all-to-all-start = ((bf16[64,2,1200]{2,1,0:T(2,128)(2,1)}), bf16[64,2,1200]{2,1,0:T(2,128)(2,1)}, u32[]{:S(2)}, u32[]{:S(2)}) async-start(bf16[64,2,1200]{2,1,0:T(2,128)(2,1)} %reshape.628), calls=%async_computation | async-start | bytes 655360 | tf_op jit(solution)/shard_map/all_to_all | solution.py:83
  46.7 13.6 %fusion.17 = (f32[640,1,1280]{2,0,1:T(8,128)S(1)}, f32[640,1,1280]{2,0,1:T(8,128)S(1)}) fusion(s32[640]{0:T(1024)S(1)} %copy-done.85), kind=kLoop, calls=%fused_computation.21 | loop fusion | flops 8192000 | bytes 6556160 | tf_op jit(solution)/shard_map/cos | solution.py:27
  61.0 3.4 copy.1087
  64.4 3.3 reshape.620
  67.7 3.3 convert_element_type.96
  71.0 7.8 reshape.629
  78.9 3.9 bitcast_bitcast_fusion.5
  82.8 13.6 %copy.1090 = bf16[64,10,2,12,1,10]{5,3,2,1,0,4:T(8,128)(2,1)} copy(bf16[64,10,2,12,1,10]{3,2,5,1,0,4:T(2,128)(2,1)} %bitcast_bitcast_fusion.5) | data formatting | bytes 614400 | tf_op jit(solution)/shard_map/all_to_all | solution.py:83
  96.4 7.1 reshape.603
  200.0 14.6 %copy.1158 = bf16[64,10,2,12,1,10]{3,2,5,4,1,0:T(2,128)(2,1)S(1)} copy(bf16[64,10,2,12,1,10]{5,3,2,1,4,0:T(8,128)(2,1)} %constant_dynamic-update-slice_fusion) | data formatting | bytes 614400 | tf_op jit(solution)/shard_map/stack | solution.py:86
  214.6 4.6 reshape.630
  219.2 23.5 %all_to_all.60 = bf16[64,2,1200]{2,1,0:T(2,128)(2,1)} all-to-all(bf16[64,2,1200]{2,1,0:T(2,128)(2,1)} %reshape.630), channel_id=1, replica_groups=mesh['band_0'=8,'band_1'=4,'band_2'=2,'field'=4] {'band_0','band_1','ban..., dimensions={0} | all-to-all | bytes 614400 | tf_op jit(solution)/shard_map/all_to_all | solution.py:86
  242.7 7.8 reshape.631
  250.5 3.9 bitcast_bitcast_fusion.4
  254.5 14.8 %copy.1312 = bf16[10,2,12,64,1,10]{5,3,2,1,0,4:T(8,128)(2,1)} copy(bf16[10,2,12,64,1,10]{2,1,5,4,0,3:T(2,128)(2,1)} %bitcast_bitcast_fusion.4) | data formatting | bytes 614400 | tf_op jit(solution)/shard_map/reshape.154
  269.3 6.6 reshape.623
  275.9 6.5 fusion.66
  282.4 16.0 %all-reduce.2 = (f32[]{:T(128)}, f32[]{:T(128)}) all-reduce(f32[]{:T(128)} %get-tuple-element.19, f32[]{:T(128)} %get-tuple-element.18), channel_id=1, replica_groups=mesh['band_0'=8,'band_1'=4,'band_2'=2,'field'=4] {'band_0'}, use_global_device_ids=true, to_apply=%region_1.2 | all-reduce | flops 2 | bytes 16 | tf_op jit(solution)/shard_map/psum | solution.py:15
  298.4 10.6 all-reduce.8
  312.0 11.3 %all-reduce.5 = (f32[]{:T(128)}, f32[]{:T(128)}) all-reduce(f32[]{:T(128)} %get-tuple-element.42, f32[]{:T(128)} %get-tuple-element.43), channel_id=1, replica_groups=mesh['band_0'=8,'band_1'=4,'band_2'=2,'field'=4] {'field'}, use_global_device_ids=true, to_apply=%region_4.5 | all-reduce | flops 2 | bytes 16 | tf_op jit(solution)/shard_map/psum | solution.py:15
  324.7 4.7 fusion.52
  329.4 9.7 reshape.624
  339.2 14.6 %copy.1162 = bf16[10,2,12,64,10]{2,1,4,0,3:T(2,128)(2,1)} copy(bf16[10,2,12,64,10]{4,3,2,1,0:T(8,128)(2,1)} %reshape.624) | data formatting | bytes 614400 | tf_op jit(solution)/shard_map/reshape | solution.py:82
  353.7 7.0 reshape.632
  360.7 19.1 %all_to_all.61 = bf16[64,2,1200]{2,1,0:T(2,128)(2,1)S(1)} all-to-all(bf16[64,2,1200]{2,1,0:T(2,128)(2,1)S(1)} %reshape.632), channel_id=1, replica_groups=mesh['band_0'=8,'band_1'=4,'band_2'=2,'field'=4] {'band_0','band_1','ban..., dimensions={0} | all-to-all | bytes 614400 | tf_op jit(solution)/shard_map/all_to_all | solution.py:83
  379.8 3.9 reshape.633
  383.7 5.9 bitcast_bitcast_fusion.3
  389.6 13.2 %copy.1163 = bf16[64,10,2,12,1,10]{5,3,2,1,0,4:T(8,128)(2,1)} copy(bf16[64,10,2,12,1,10]{3,2,5,1,0,4:T(2,128)(2,1)} %bitcast_bitcast_fusion.3) | data formatting | bytes 614400 | tf_op jit(solution)/shard_map/all_to_all | solution.py:83
  402.8 6.8 reshape.609
  556.5 13.2 %copy.1231 = bf16[64,10,2,12,1,10]{3,2,5,4,1,0:T(2,128)(2,1)} copy(bf16[64,10,2,12,1,10]{5,3,2,1,4,0:T(8,128)(2,1)} %constant_dynamic-update-slice_fusion.64) | data formatting | bytes 614400 | tf_op jit(solution)/shard_map/stack | solution.py:86
  569.7 7.2 reshape.634
  576.9 19.0 %all_to_all.62 = bf16[64,2,1200]{2,1,0:T(2,128)(2,1)S(1)} all-to-all(bf16[64,2,1200]{2,1,0:T(2,128)(2,1)S(1)} %reshape.634), channel_id=1, replica_groups=mesh['band_0'=8,'band_1'=4,'band_2'=2,'field'=4] {'band_0','band_1','ban..., dimensions={0} | all-to-all | bytes 614400 | tf_op jit(solution)/shard_map/all_to_all | solution.py:86
  595.9 3.9 reshape.635
  599.8 5.9 bitcast_bitcast_fusion.2
  605.7 14.7 %copy.1315 = bf16[10,2,12,64,1,10]{5,3,2,1,0,4:T(8,128)(2,1)} copy(bf16[10,2,12,64,1,10]{2,1,5,4,0,3:T(2,128)(2,1)} %bitcast_bitcast_fusion.2) | data formatting | bytes 614400 | tf_op jit(solution)/shard_map/reshape.287
  620.4 6.6 reshape.625
  627.1 7.4 multiply_reduce_fusion.2
  634.5 16.0 %all-reduce.1 = (f32[]{:T(128)}, f32[]{:T(128)}) all-reduce(f32[]{:T(128)} %get-tuple-element.17, f32[]{:T(128)} %get-tuple-element.16), channel_id=1, replica_groups=mesh['band_0'=8,'band_1'=4,'band_2'=2,'field'=4] {'band_0'}, use_global_device_ids=true, to_apply=%region_11.12 | all-reduce | flops 2 | bytes 16 | tf_op jit(solution)/shard_map/psum | solution.py:15
  650.5 10.6 all-reduce.7
  664.1 8.6 all-reduce.4
  678.5 5.5 fusion.55
  684.0 10.4 reshape.626
  694.4 14.6 %copy.1235 = bf16[10,2,12,64,10]{2,1,4,0,3:T(2,128)(2,1)} copy(bf16[10,2,12,64,10]{4,3,2,1,0:T(8,128)(2,1)} %reshape.626) | data formatting | bytes 614400 | tf_op jit(solution)/shard_map/reshape | solution.py:82
  708.9 7.6 reshape.636
  716.5 19.4 %all_to_all.63 = bf16[64,2,1200]{2,1,0:T(2,128)(2,1)} all-to-all(bf16[64,2,1200]{2,1,0:T(2,128)(2,1)} %reshape.636), channel_id=1, replica_groups=mesh['band_0'=8,'band_1'=4,'band_2'=2,'field'=4] {'band_0','band_1','ban..., dimensions={0} | all-to-all | bytes 614400 | tf_op jit(solution)/shard_map/all_to_all | solution.py:83
  735.9 8.6 reshape.637
  744.6 5.9 bitcast_bitcast_fusion.1
  750.4 13.2 %copy.1236 = bf16[64,10,2,12,1,10]{5,3,2,1,0,4:T(8,128)(2,1)} copy(bf16[64,10,2,12,1,10]{3,2,5,1,0,4:T(2,128)(2,1)} %bitcast_bitcast_fusion.1) | data formatting | bytes 614400 | tf_op jit(solution)/shard_map/all_to_all | solution.py:83
  763.7 7.5 reshape.615
  946.5 13.2 %copy.1304 = bf16[64,10,2,12,1,10]{3,2,5,4,1,0:T(2,128)(2,1)} copy(bf16[64,10,2,12,1,10]{5,3,2,1,4,0:T(8,128)(2,1)} %constant_dynamic-update-slice_fusion.128) | data formatting | bytes 614400 | tf_op jit(solution)/shard_map/stack | solution.py:86
  959.8 7.8 reshape.638
  967.5 19.3 %all_to_all.64 = bf16[64,2,1200]{2,1,0:T(2,128)(2,1)} all-to-all(bf16[64,2,1200]{2,1,0:T(2,128)(2,1)} %reshape.638), channel_id=1, replica_groups=mesh['band_0'=8,'band_1'=4,'band_2'=2,'field'=4] {'band_0','band_1','ban..., dimensions={0} | all-to-all | bytes 614400 | tf_op jit(solution)/shard_map/all_to_all | solution.py:86
  986.9 8.6 reshape.639
  995.5 5.9 bitcast_bitcast_fusion
  1001.3 14.7 %copy.1318 = bf16[10,2,12,64,1,10]{5,3,2,1,0,4:T(8,128)(2,1)} copy(bf16[10,2,12,64,1,10]{2,1,5,4,0,3:T(2,128)(2,1)} %bitcast_bitcast_fusion) | data formatting | bytes 614400 | tf_op jit(solution)/shard_map/reshape.420
  1016.1 7.3 reshape.627
  1023.3 7.6 multiply_reduce_fusion
  1030.9 16.0 %all-reduce = (f32[]{:T(128)}, f32[]{:T(128)}) all-reduce(f32[]{:T(128)} %get-tuple-element.15, f32[]{:T(128)} %get-tuple-element.14), channel_id=1, replica_groups=mesh['band_0'=8,'band_1'=4,'band_2'=2,'field'=4] {'band_0'}, use_global_device_ids=true, to_apply=%region_21.22 | all-reduce | flops 2 | bytes 16 | tf_op jit(solution)/shard_map/psum | solution.py:15
  1046.9 10.6 all-reduce.6
  1060.6 10.3 all-reduce.3
  (796 shorter events, 434.3 us)
Async XLA Ops:
  34.6 36.5 %all-to-all-start = ((bf16[64,2,1200]{2,1,0:T(2,128)(2,1)}), bf16[64,2,1200]{2,1,0:T(2,128)(2,1)}, u32[]{:S(2)}, u32[]{:S(2)}) async-start(bf16[64,2,1200]{2,1,0:T(2,128)(2,1)} %reshape.628), calls=%async_computation | async-start | bytes 655360 | tf_op jit(solution)/shard_map/all_to_all | solution.py:83
  159.8 38.2 %copy-start.76 = (bf16[1,10,2,12,1,10]{5,3,2,1,4,0:T(8,128)(2,1)S(1)}, bf16[1,10,2,12,1,10]{5,3,2,1,4,0:T(8,128)(2,1)}, u32[]{:S(2)}) copy-start(bf16[1,10,2,12,1,10]{5,3,2,1,4,0:T(8,128)(2,1)} %stack.652) | copy-start | bytes 14404
  159.9 38.9 %copy-start.79 = (bf16[1,10,2,12,1,10]{5,3,2,1,4,0:T(8,128)(2,1)S(1)}, bf16[1,10,2,12,1,10]{5,3,2,1,4,0:T(8,128)(2,1)}, u32[]{:S(2)}) copy-start(bf16[1,10,2,12,1,10]{5,3,2,1,4,0:T(8,128)(2,1)} %stack.653) | copy-start | bytes 14404
  159.9 39.5 %copy-start.82 = (bf16[1,10,2,12,1,10]{5,3,2,1,4,0:T(8,128)(2,1)S(1)}, bf16[1,10,2,12,1,10]{5,3,2,1,4,0:T(8,128)(2,1)}, u32[]{:S(2)}) copy-start(bf16[1,10,2,12,1,10]{5,3,2,1,4,0:T(8,128)(2,1)} %stack.654) | copy-start | bytes 14404
  500.1 37.8 %copy-start.6 = (bf16[1,10,2,12,1,10]{5,3,2,1,4,0:T(8,128)(2,1)S(1)}, bf16[1,10,2,12,1,10]{5,3,2,1,4,0:T(8,128)(2,1)}, u32[]{:S(2)}) copy-start(bf16[1,10,2,12,1,10]{5,3,2,1,4,0:T(8,128)(2,1)} %stack.691) | copy-start | bytes 14404
  500.1 38.4 %copy-start.8 = (bf16[1,10,2,12,1,10]{5,3,2,1,4,0:T(8,128)(2,1)S(1)}, bf16[1,10,2,12,1,10]{5,3,2,1,4,0:T(8,128)(2,1)}, u32[]{:S(2)}) copy-start(bf16[1,10,2,12,1,10]{5,3,2,1,4,0:T(8,128)(2,1)} %stack.692) | copy-start | bytes 14404
  500.1 39.1 %copy-start.10 = (bf16[1,10,2,12,1,10]{5,3,2,1,4,0:T(8,128)(2,1)S(1)}, bf16[1,10,2,12,1,10]{5,3,2,1,4,0:T(8,128)(2,1)}, u32[]{:S(2)}) copy-start(bf16[1,10,2,12,1,10]{5,3,2,1,4,0:T(8,128)(2,1)} %stack.693) | copy-start | bytes 14404
  500.1 39.7 %copy-start.12 = (bf16[1,10,2,12,1,10]{5,3,2,1,4,0:T(8,128)(2,1)S(1)}, bf16[1,10,2,12,1,10]{5,3,2,1,4,0:T(8,128)(2,1)}, u32[]{:S(2)}) copy-start(bf16[1,10,2,12,1,10]{5,3,2,1,4,0:T(8,128)(2,1)} %stack.694) | copy-start | bytes 14404
  500.1 40.3 %copy-start.14 = (bf16[1,10,2,12,1,10]{5,3,2,1,4,0:T(8,128)(2,1)S(1)}, bf16[1,10,2,12,1,10]{5,3,2,1,4,0:T(8,128)(2,1)}, u32[]{:S(2)}) copy-start(bf16[1,10,2,12,1,10]{5,3,2,1,4,0:T(8,128)(2,1)} %stack.695) | copy-start | bytes 14404
  500.2 41.0 %copy-start.16 = (bf16[1,10,2,12,1,10]{5,3,2,1,4,0:T(8,128)(2,1)S(1)}, bf16[1,10,2,12,1,10]{5,3,2,1,4,0:T(8,128)(2,1)}, u32[]{:S(2)}) copy-start(bf16[1,10,2,12,1,10]{5,3,2,1,4,0:T(8,128)(2,1)} %stack.696) | copy-start | bytes 14404
  500.2 41.6 %copy-start.18 = (bf16[1,10,2,12,1,10]{5,3,2,1,4,0:T(8,128)(2,1)S(1)}, bf16[1,10,2,12,1,10]{5,3,2,1,4,0:T(8,128)(2,1)}, u32[]{:S(2)}) copy-start(bf16[1,10,2,12,1,10]{5,3,2,1,4,0:T(8,128)(2,1)} %stack.697) | copy-start | bytes 14404
  500.2 42.2 %copy-start.20 = (bf16[1,10,2,12,1,10]{5,3,2,1,4,0:T(8,128)(2,1)S(1)}, bf16[1,10,2,12,1,10]{5,3,2,1,4,0:T(8,128)(2,1)}, u32[]{:S(2)}) copy-start(bf16[1,10,2,12,1,10]{5,3,2,1,4,0:T(8,128)(2,1)} %stack.698) | copy-start | bytes 14404
  500.2 42.8 %copy-start.23 = (bf16[1,10,2,12,1,10]{5,3,2,1,4,0:T(8,128)(2,1)S(1)}, bf16[1,10,2,12,1,10]{5,3,2,1,4,0:T(8,128)(2,1)}, u32[]{:S(2)}) copy-start(bf16[1,10,2,12,1,10]{5,3,2,1,4,0:T(8,128)(2,1)} %stack.699) | copy-start | bytes 14404
  500.2 43.5 %copy-start.26 = (bf16[1,10,2,12,1,10]{5,3,2,1,4,0:T(8,128)(2,1)S(1)}, bf16[1,10,2,12,1,10]{5,3,2,1,4,0:T(8,128)(2,1)}, u32[]{:S(2)}) copy-start(bf16[1,10,2,12,1,10]{5,3,2,1,4,0:T(8,128)(2,1)} %stack.700) | copy-start | bytes 14404
  500.2 44.1 %copy-start.29 = (bf16[1,10,2,12,1,10]{5,3,2,1,4,0:T(8,128)(2,1)S(1)}, bf16[1,10,2,12,1,10]{5,3,2,1,4,0:T(8,128)(2,1)}, u32[]{:S(2)}) copy-start(bf16[1,10,2,12,1,10]{5,3,2,1,4,0:T(8,128)(2,1)} %stack.701) | copy-start | bytes 14404
  500.2 44.7 %copy-start.32 = (bf16[1,10,2,12,1,10]{5,3,2,1,4,0:T(8,128)(2,1)S(1)}, bf16[1,10,2,12,1,10]{5,3,2,1,4,0:T(8,128)(2,1)}, u32[]{:S(2)}) copy-start(bf16[1,10,2,12,1,10]{5,3,2,1,4,0:T(8,128)(2,1)} %stack.702) | copy-start | bytes 14404
  500.2 45.4 %copy-start.35 = (bf16[1,10,2,12,1,10]{5,3,2,1,4,0:T(8,128)(2,1)S(1)}, bf16[1,10,2,12,1,10]{5,3,2,1,4,0:T(8,128)(2,1)}, u32[]{:S(2)}) copy-start(bf16[1,10,2,12,1,10]{5,3,2,1,4,0:T(8,128)(2,1)} %stack.703) | copy-start | bytes 14404
  500.2 46.0 %copy-start.38 = (bf16[1,10,2,12,1,10]{5,3,2,1,4,0:T(8,128)(2,1)S(1)}, bf16[1,10,2,12,1,10]{5,3,2,1,4,0:T(8,128)(2,1)}, u32[]{:S(2)}) copy-start(bf16[1,10,2,12,1,10]{5,3,2,1,4,0:T(8,128)(2,1)} %stack.704) | copy-start | bytes 14404
  500.2 46.6 %copy-start.41 = (bf16[1,10,2,12,1,10]{5,3,2,1,4,0:T(8,128)(2,1)S(1)}, bf16[1,10,2,12,1,10]{5,3,2,1,4,0:T(8,128)(2,1)}, u32[]{:S(2)}) copy-start(bf16[1,10,2,12,1,10]{5,3,2,1,4,0:T(8,128)(2,1)} %stack.705) | copy-start | bytes 14404
  500.3 47.3 %copy-start.44 = (bf16[1,10,2,12,1,10]{5,3,2,1,4,0:T(8,128)(2,1)S(1)}, bf16[1,10,2,12,1,10]{5,3,2,1,4,0:T(8,128)(2,1)}, u32[]{:S(2)}) copy-start(bf16[1,10,2,12,1,10]{5,3,2,1,4,0:T(8,128)(2,1)} %stack.706) | copy-start | bytes 14404
  500.3 47.9 %copy-start.47 = (bf16[1,10,2,12,1,10]{5,3,2,1,4,0:T(8,128)(2,1)S(1)}, bf16[1,10,2,12,1,10]{5,3,2,1,4,0:T(8,128)(2,1)}, u32[]{:S(2)}) copy-start(bf16[1,10,2,12,1,10]{5,3,2,1,4,0:T(8,128)(2,1)} %stack.707) | copy-start | bytes 14404
  500.3 48.5 %copy-start.50 = (bf16[1,10,2,12,1,10]{5,3,2,1,4,0:T(8,128)(2,1)S(1)}, bf16[1,10,2,12,1,10]{5,3,2,1,4,0:T(8,128)(2,1)}, u32[]{:S(2)}) copy-start(bf16[1,10,2,12,1,10]{5,3,2,1,4,0:T(8,128)(2,1)} %stack.708) | copy-start | bytes 14404
  500.3 49.1 %copy-start.53 = (bf16[1,10,2,12,1,10]{5,3,2,1,4,0:T(8,128)(2,1)S(1)}, bf16[1,10,2,12,1,10]{5,3,2,1,4,0:T(8,128)(2,1)}, u32[]{:S(2)}) copy-start(bf16[1,10,2,12,1,10]{5,3,2,1,4,0:T(8,128)(2,1)} %stack.709) | copy-start | bytes 14404
  500.3 49.8 %copy-start.56 = (bf16[1,10,2,12,1,10]{5,3,2,1,4,0:T(8,128)(2,1)S(1)}, bf16[1,10,2,12,1,10]{5,3,2,1,4,0:T(8,128)(2,1)}, u32[]{:S(2)}) copy-start(bf16[1,10,2,12,1,10]{5,3,2,1,4,0:T(8,128)(2,1)} %stack.710) | copy-start | bytes 14404
  500.3 50.4 %copy-start.59 = (bf16[1,10,2,12,1,10]{5,3,2,1,4,0:T(8,128)(2,1)S(1)}, bf16[1,10,2,12,1,10]{5,3,2,1,4,0:T(8,128)(2,1)}, u32[]{:S(2)}) copy-start(bf16[1,10,2,12,1,10]{5,3,2,1,4,0:T(8,128)(2,1)} %stack.711) | copy-start | bytes 14404
  500.3 51.0 %copy-start.62 = (bf16[1,10,2,12,1,10]{5,3,2,1,4,0:T(8,128)(2,1)S(1)}, bf16[1,10,2,12,1,10]{5,3,2,1,4,0:T(8,128)(2,1)}, u32[]{:S(2)}) copy-start(bf16[1,10,2,12,1,10]{5,3,2,1,4,0:T(8,128)(2,1)} %stack.712) | copy-start | bytes 14404
  500.3 51.7 %copy-start.65 = (bf16[1,10,2,12,1,10]{5,3,2,1,4,0:T(8,128)(2,1)S(1)}, bf16[1,10,2,12,1,10]{5,3,2,1,4,0:T(8,128)(2,1)}, u32[]{:S(2)}) copy-start(bf16[1,10,2,12,1,10]{5,3,2,1,4,0:T(8,128)(2,1)} %stack.713) | copy-start | bytes 14404
  500.3 52.3 %copy-start.68 = (bf16[1,10,2,12,1,10]{5,3,2,1,4,0:T(8,128)(2,1)S(1)}, bf16[1,10,2,12,1,10]{5,3,2,1,4,0:T(8,128)(2,1)}, u32[]{:S(2)}) copy-start(bf16[1,10,2,12,1,10]{5,3,2,1,4,0:T(8,128)(2,1)} %stack.714) | copy-start | bytes 14404
  500.3 52.9 %copy-start.71 = (bf16[1,10,2,12,1,10]{5,3,2,1,4,0:T(8,128)(2,1)S(1)}, bf16[1,10,2,12,1,10]{5,3,2,1,4,0:T(8,128)(2,1)}, u32[]{:S(2)}) copy-start(bf16[1,10,2,12,1,10]{5,3,2,1,4,0:T(8,128)(2,1)} %stack.715) | copy-start | bytes 14404
  500.4 53.6 %copy-start.74 = (bf16[1,10,2,12,1,10]{5,3,2,1,4,0:T(8,128)(2,1)S(1)}, bf16[1,10,2,12,1,10]{5,3,2,1,4,0:T(8,128)(2,1)}, u32[]{:S(2)}) copy-start(bf16[1,10,2,12,1,10]{5,3,2,1,4,0:T(8,128)(2,1)} %stack.716) | copy-start | bytes 14404
  500.4 54.2 %copy-start.77 = (bf16[1,10,2,12,1,10]{5,3,2,1,4,0:T(8,128)(2,1)S(1)}, bf16[1,10,2,12,1,10]{5,3,2,1,4,0:T(8,128)(2,1)}, u32[]{:S(2)}) copy-start(bf16[1,10,2,12,1,10]{5,3,2,1,4,0:T(8,128)(2,1)} %stack.717) | copy-start | bytes 14404
  500.4 54.8 %copy-start.80 = (bf16[1,10,2,12,1,10]{5,3,2,1,4,0:T(8,128)(2,1)S(1)}, bf16[1,10,2,12,1,10]{5,3,2,1,4,0:T(8,128)(2,1)}, u32[]{:S(2)}) copy-start(bf16[1,10,2,12,1,10]{5,3,2,1,4,0:T(8,128)(2,1)} %stack.718) | copy-start | bytes 14404
  500.4 55.5 %copy-start.83 = (bf16[1,10,2,12,1,10]{5,3,2,1,4,0:T(8,128)(2,1)S(1)}, bf16[1,10,2,12,1,10]{5,3,2,1,4,0:T(8,128)(2,1)}, u32[]{:S(2)}) copy-start(bf16[1,10,2,12,1,10]{5,3,2,1,4,0:T(8,128)(2,1)} %stack.719) | copy-start | bytes 14404
  881.3 45.4 %copy-start.3 = (bf16[1,10,2,12,1,10]{5,3,2,1,4,0:T(8,128)(2,1)S(1)}, bf16[1,10,2,12,1,10]{5,3,2,1,4,0:T(8,128)(2,1)}, u32[]{:S(2)}) copy-start(bf16[1,10,2,12,1,10]{5,3,2,1,4,0:T(8,128)(2,1)} %stack.754) | copy-start | bytes 14404
  881.3 46.0 %copy-start.5 = (bf16[1,10,2,12,1,10]{5,3,2,1,4,0:T(8,128)(2,1)S(1)}, bf16[1,10,2,12,1,10]{5,3,2,1,4,0:T(8,128)(2,1)}, u32[]{:S(2)}) copy-start(bf16[1,10,2,12,1,10]{5,3,2,1,4,0:T(8,128)(2,1)} %stack.755) | copy-start | bytes 14404
  881.3 46.7 %copy-start.7 = (bf16[1,10,2,12,1,10]{5,3,2,1,4,0:T(8,128)(2,1)S(1)}, bf16[1,10,2,12,1,10]{5,3,2,1,4,0:T(8,128)(2,1)}, u32[]{:S(2)}) copy-start(bf16[1,10,2,12,1,10]{5,3,2,1,4,0:T(8,128)(2,1)} %stack.756) | copy-start | bytes 14404
  881.3 47.3 %copy-start.9 = (bf16[1,10,2,12,1,10]{5,3,2,1,4,0:T(8,128)(2,1)S(1)}, bf16[1,10,2,12,1,10]{5,3,2,1,4,0:T(8,128)(2,1)}, u32[]{:S(2)}) copy-start(bf16[1,10,2,12,1,10]{5,3,2,1,4,0:T(8,128)(2,1)} %stack.757) | copy-start | bytes 14404
  881.3 47.9 %copy-start.11 = (bf16[1,10,2,12,1,10]{5,3,2,1,4,0:T(8,128)(2,1)S(1)}, bf16[1,10,2,12,1,10]{5,3,2,1,4,0:T(8,128)(2,1)}, u32[]{:S(2)}) copy-start(bf16[1,10,2,12,1,10]{5,3,2,1,4,0:T(8,128)(2,1)} %stack.758) | copy-start | bytes 14404
  881.3 48.6 %copy-start.13 = (bf16[1,10,2,12,1,10]{5,3,2,1,4,0:T(8,128)(2,1)S(1)}, bf16[1,10,2,12,1,10]{5,3,2,1,4,0:T(8,128)(2,1)}, u32[]{:S(2)}) copy-start(bf16[1,10,2,12,1,10]{5,3,2,1,4,0:T(8,128)(2,1)} %stack.759) | copy-start | bytes 14404
  881.3 49.2 %copy-start.15 = (bf16[1,10,2,12,1,10]{5,3,2,1,4,0:T(8,128)(2,1)S(1)}, bf16[1,10,2,12,1,10]{5,3,2,1,4,0:T(8,128)(2,1)}, u32[]{:S(2)}) copy-start(bf16[1,10,2,12,1,10]{5,3,2,1,4,0:T(8,128)(2,1)} %stack.760) | copy-start | bytes 14404
  881.3 49.8 %copy-start.17 = (bf16[1,10,2,12,1,10]{5,3,2,1,4,0:T(8,128)(2,1)S(1)}, bf16[1,10,2,12,1,10]{5,3,2,1,4,0:T(8,128)(2,1)}, u32[]{:S(2)}) copy-start(bf16[1,10,2,12,1,10]{5,3,2,1,4,0:T(8,128)(2,1)} %stack.761) | copy-start | bytes 14404
  881.3 50.4 %copy-start.19 = (bf16[1,10,2,12,1,10]{5,3,2,1,4,0:T(8,128)(2,1)S(1)}, bf16[1,10,2,12,1,10]{5,3,2,1,4,0:T(8,128)(2,1)}, u32[]{:S(2)}) copy-start(bf16[1,10,2,12,1,10]{5,3,2,1,4,0:T(8,128)(2,1)} %stack.762) | copy-start | bytes 14404
  881.4 51.1 %copy-start.21 = (bf16[1,10,2,12,1,10]{5,3,2,1,4,0:T(8,128)(2,1)S(1)}, bf16[1,10,2,12,1,10]{5,3,2,1,4,0:T(8,128)(2,1)}, u32[]{:S(2)}) copy-start(bf16[1,10,2,12,1,10]{5,3,2,1,4,0:T(8,128)(2,1)} %stack.763) | copy-start | bytes 14404
  881.4 51.7 %copy-start.24 = (bf16[1,10,2,12,1,10]{5,3,2,1,4,0:T(8,128)(2,1)S(1)}, bf16[1,10,2,12,1,10]{5,3,2,1,4,0:T(8,128)(2,1)}, u32[]{:S(2)}) copy-start(bf16[1,10,2,12,1,10]{5,3,2,1,4,0:T(8,128)(2,1)} %stack.764) | copy-start | bytes 14404
  881.4 52.3 %copy-start.27 = (bf16[1,10,2,12,1,10]{5,3,2,1,4,0:T(8,128)(2,1)S(1)}, bf16[1,10,2,12,1,10]{5,3,2,1,4,0:T(8,128)(2,1)}, u32[]{:S(2)}) copy-start(bf16[1,10,2,12,1,10]{5,3,2,1,4,0:T(8,128)(2,1)} %stack.765) | copy-start | bytes 14404
  881.4 53.0 %copy-start.30 = (bf16[1,10,2,12,1,10]{5,3,2,1,4,0:T(8,128)(2,1)S(1)}, bf16[1,10,2,12,1,10]{5,3,2,1,4,0:T(8,128)(2,1)}, u32[]{:S(2)}) copy-start(bf16[1,10,2,12,1,10]{5,3,2,1,4,0:T(8,128)(2,1)} %stack.766) | copy-start | bytes 14404
  881.4 53.6 %copy-start.33 = (bf16[1,10,2,12,1,10]{5,3,2,1,4,0:T(8,128)(2,1)S(1)}, bf16[1,10,2,12,1,10]{5,3,2,1,4,0:T(8,128)(2,1)}, u32[]{:S(2)}) copy-start(bf16[1,10,2,12,1,10]{5,3,2,1,4,0:T(8,128)(2,1)} %stack.767) | copy-start | bytes 14404
  881.4 54.2 %copy-start.36 = (bf16[1,10,2,12,1,10]{5,3,2,1,4,0:T(8,128)(2,1)S(1)}, bf16[1,10,2,12,1,10]{5,3,2,1,4,0:T(8,128)(2,1)}, u32[]{:S(2)}) copy-start(bf16[1,10,2,12,1,10]{5,3,2,1,4,0:T(8,128)(2,1)} %stack.768) | copy-start | bytes 14404
  881.4 54.9 %copy-start.39 = (bf16[1,10,2,12,1,10]{5,3,2,1,4,0:T(8,128)(2,1)S(1)}, bf16[1,10,2,12,1,10]{5,3,2,1,4,0:T(8,128)(2,1)}, u32[]{:S(2)}) copy-start(bf16[1,10,2,12,1,10]{5,3,2,1,4,0:T(8,128)(2,1)} %stack.769) | copy-start | bytes 14404
  881.4 55.5 %copy-start.42 = (bf16[1,10,2,12,1,10]{5,3,2,1,4,0:T(8,128)(2,1)S(1)}, bf16[1,10,2,12,1,10]{5,3,2,1,4,0:T(8,128)(2,1)}, u32[]{:S(2)}) copy-start(bf16[1,10,2,12,1,10]{5,3,2,1,4,0:T(8,128)(2,1)} %stack.770) | copy-start | bytes 14404
  881.4 56.1 %copy-start.45 = (bf16[1,10,2,12,1,10]{5,3,2,1,4,0:T(8,128)(2,1)S(1)}, bf16[1,10,2,12,1,10]{5,3,2,1,4,0:T(8,128)(2,1)}, u32[]{:S(2)}) copy-start(bf16[1,10,2,12,1,10]{5,3,2,1,4,0:T(8,128)(2,1)} %stack.771) | copy-start | bytes 14404
  881.4 56.7 %copy-start.48 = (bf16[1,10,2,12,1,10]{5,3,2,1,4,0:T(8,128)(2,1)S(1)}, bf16[1,10,2,12,1,10]{5,3,2,1,4,0:T(8,128)(2,1)}, u32[]{:S(2)}) copy-start(bf16[1,10,2,12,1,10]{5,3,2,1,4,0:T(8,128)(2,1)} %stack.772) | copy-start | bytes 14404
  881.5 57.4 %copy-start.51 = (bf16[1,10,2,12,1,10]{5,3,2,1,4,0:T(8,128)(2,1)S(1)}, bf16[1,10,2,12,1,10]{5,3,2,1,4,0:T(8,128)(2,1)}, u32[]{:S(2)}) copy-start(bf16[1,10,2,12,1,10]{5,3,2,1,4,0:T(8,128)(2,1)} %stack.773) | copy-start | bytes 14404
  881.5 58.0 %copy-start.54 = (bf16[1,10,2,12,1,10]{5,3,2,1,4,0:T(8,128)(2,1)S(1)}, bf16[1,10,2,12,1,10]{5,3,2,1,4,0:T(8,128)(2,1)}, u32[]{:S(2)}) copy-start(bf16[1,10,2,12,1,10]{5,3,2,1,4,0:T(8,128)(2,1)} %stack.774) | copy-start | bytes 14404
  881.5 58.6 %copy-start.57 = (bf16[1,10,2,12,1,10]{5,3,2,1,4,0:T(8,128)(2,1)S(1)}, bf16[1,10,2,12,1,10]{5,3,2,1,4,0:T(8,128)(2,1)}, u32[]{:S(2)}) copy-start(bf16[1,10,2,12,1,10]{5,3,2,1,4,0:T(8,128)(2,1)} %stack.775) | copy-start | bytes 14404
  881.5 59.3 %copy-start.60 = (bf16[1,10,2,12,1,10]{5,3,2,1,4,0:T(8,128)(2,1)S(1)}, bf16[1,10,2,12,1,10]{5,3,2,1,4,0:T(8,128)(2,1)}, u32[]{:S(2)}) copy-start(bf16[1,10,2,12,1,10]{5,3,2,1,4,0:T(8,128)(2,1)} %stack.776) | copy-start | bytes 14404
  881.5 59.9 %copy-start.63 = (bf16[1,10,2,12,1,10]{5,3,2,1,4,0:T(8,128)(2,1)S(1)}, bf16[1,10,2,12,1,10]{5,3,2,1,4,0:T(8,128)(2,1)}, u32[]{:S(2)}) copy-start(bf16[1,10,2,12,1,10]{5,3,2,1,4,0:T(8,128)(2,1)} %stack.777) | copy-start | bytes 14404
  881.5 60.5 %copy-start.66 = (bf16[1,10,2,12,1,10]{5,3,2,1,4,0:T(8,128)(2,1)S(1)}, bf16[1,10,2,12,1,10]{5,3,2,1,4,0:T(8,128)(2,1)}, u32[]{:S(2)}) copy-start(bf16[1,10,2,12,1,10]{5,3,2,1,4,0:T(8,128)(2,1)} %stack.778) | copy-start | bytes 14404
  881.5 61.2 %copy-start.69 = (bf16[1,10,2,12,1,10]{5,3,2,1,4,0:T(8,128)(2,1)S(1)}, bf16[1,10,2,12,1,10]{5,3,2,1,4,0:T(8,128)(2,1)}, u32[]{:S(2)}) copy-start(bf16[1,10,2,12,1,10]{5,3,2,1,4,0:T(8,128)(2,1)} %stack.779) | copy-start | bytes 14404
  881.5 61.8 %copy-start.72 = (bf16[1,10,2,12,1,10]{5,3,2,1,4,0:T(8,128)(2,1)S(1)}, bf16[1,10,2,12,1,10]{5,3,2,1,4,0:T(8,128)(2,1)}, u32[]{:S(2)}) copy-start(bf16[1,10,2,12,1,10]{5,3,2,1,4,0:T(8,128)(2,1)} %stack.780) | copy-start | bytes 14404
  881.5 62.4 %copy-start.75 = (bf16[1,10,2,12,1,10]{5,3,2,1,4,0:T(8,128)(2,1)S(1)}, bf16[1,10,2,12,1,10]{5,3,2,1,4,0:T(8,128)(2,1)}, u32[]{:S(2)}) copy-start(bf16[1,10,2,12,1,10]{5,3,2,1,4,0:T(8,128)(2,1)} %stack.781) | copy-start | bytes 14404
  881.5 63.1 %copy-start.78 = (bf16[1,10,2,12,1,10]{5,3,2,1,4,0:T(8,128)(2,1)S(1)}, bf16[1,10,2,12,1,10]{5,3,2,1,4,0:T(8,128)(2,1)}, u32[]{:S(2)}) copy-start(bf16[1,10,2,12,1,10]{5,3,2,1,4,0:T(8,128)(2,1)} %stack.782) | copy-start | bytes 14404
  881.6 63.7 %copy-start.81 = (bf16[1,10,2,12,1,10]{5,3,2,1,4,0:T(8,128)(2,1)S(1)}, bf16[1,10,2,12,1,10]{5,3,2,1,4,0:T(8,128)(2,1)}, u32[]{:S(2)}) copy-start(bf16[1,10,2,12,1,10]{5,3,2,1,4,0:T(8,128)(2,1)} %stack.783) | copy-start | bytes 14404
  881.6 64.3 %copy-start.84 = (bf16[1,10,2,12,1,10]{5,3,2,1,4,0:T(8,128)(2,1)S(1)}, bf16[1,10,2,12,1,10]{5,3,2,1,4,0:T(8,128)(2,1)}, u32[]{:S(2)}) copy-start(bf16[1,10,2,12,1,10]{5,3,2,1,4,0:T(8,128)(2,1)} %stack.784) | copy-start | bytes 14404
  (26 other events, 745.3 us)
